TPU v7x, 32 devices: a whole 2x2x4 slice. The times are simulated.
32 devices in a mesh: grp: 2 (over x), ma: 16 (over z, y, core).
Axes of the slice: x: 2, y: 2, z: 4, core: 2. Of those that a mesh axis runs over, the one named last changes fastest.
Arguments:
- tbar_alm: bfloat16 [128, 8, 2, 257], P('ma', 'grp'), parts along dimension 1, may hold values from -6 to 6
- twf_alm: bfloat16 [128, 8, 2, 257], P('ma', 'grp'), parts along dimension 1, may hold values from -6 to 6
- legendre: bfloat16 [128, 257, 16], P('ma'), may hold values from -0.375 to 0.375
- m_slots: int32 [128], replicated, may hold values from 0 to 127, each once
- cycle_order: int32 [16], replicated, may hold values from 0 to 15, each once
- colatitude: float32 [16], replicated, may hold values from 0.35 to 2.79
- cycle_weight: float32 [16], replicated, may hold values from 0.25 to 1
- pixel_mask: int32 [16, 4096], P('ma'), may hold values from 0 to 3
Outputs:
- gradient: float32 [128, 8, 2, 257], P('ma', 'grp'), parts along dimension 1
- curl: float32 [128, 8, 2, 257], P('ma', 'grp'), parts along dimension 1
There are 2 independent parts, one for each index of `grp`. A program takes and returns all parts, laid end to end along the dimension named above; an argument that names none is the same for every part. Nothing has to cross between parts.
Inputs may be any that keep to these rules, and one draw needn't show every extreme that they name: Pair p holds the orders m_slots[p] and 255 - m_slots[p]; each value appears once. Cycle slot i holds cycle cycle_order[i]; each value appears once.
All inputs are finite; a program needn't handle non-finite values.
Results may differ from a plain program's by a relative error of at most 0.017.
Values may be sent and summed in bfloat16 or wider, within the bound.
A program may use at most 128 MiB of HBM per device.

v0:
```python
import math

import jax
import jax.numpy as jnp
from jax import lax
from jax.sharding import PartitionSpec as P


def pair_layout(small_orders, mode_count):
    row_index = lax.broadcasted_iota(jnp.int32, (small_orders.shape[0], mode_count + 1), 1)
    smaller = small_orders[:, None]
    upper_half = row_index >= mode_count - smaller
    degree = jnp.where(upper_half, row_index - 1, smaller + row_index)
    orders = jnp.where(upper_half, mode_count - 1 - smaller, smaller + 0 * row_index)
    return (upper_half, degree.astype(jnp.float32), orders.astype(jnp.float32))


def raising(degree, orders):
    square = (
        (degree * degree - orders * orders)
        * (2.0 * degree + 1.0)
        / jnp.maximum(2.0 * degree - 1.0, 1.0)
    )
    return jnp.where(degree > orders, jnp.sqrt(jnp.where(degree > orders, square, 0.0)), 0.0)


def synthesis_sets(tbar_alm, twf_alm, degree, raising_factor, mode_count):
    wiener = twf_alm.astype(jnp.float32)
    scaled = (raising_factor / mode_count)[:, None, None, :] * wiener
    raised = jnp.concatenate([scaled[..., 1:], jnp.zeros_like(scaled[..., :1])], axis=-1)
    stacked = jnp.stack(
        [
            tbar_alm.astype(jnp.float32),
            wiener,
            (degree / mode_count)[:, None, None, :] * wiener,
            raised,
        ],
        axis=2,
    )
    return stacked.reshape(stacked.shape[0], stacked.shape[1], 8, stacked.shape[4]).astype(
        jnp.bfloat16
    )


def mode_columns(small_orders, mode_count):
    return jnp.stack([small_orders, mode_count - 1 - small_orders], axis=1).reshape(-1)


def fourier_table(orders_int, pixel_count):
    pixel_index = lax.broadcasted_iota(jnp.int32, (orders_int.shape[0], pixel_count), 1)
    turns = orders_int[:, None] * pixel_index % pixel_count
    radians = turns.astype(jnp.float32) * (2.0 * math.pi / pixel_count)
    return jnp.stack([jnp.cos(radians), -jnp.sin(radians)], axis=0).astype(jnp.bfloat16)


def combine_modes(legendre_sums, orders_int, cos_cycle, sin_cycle, mode_count):
    orders_real = orders_int.astype(jnp.float32)
    inv_sin = 1.0 / sin_cycle
    ratio = (orders_real / mode_count)[:, None]
    theta_real = (cos_cycle * legendre_sums[:, 4] - legendre_sums[:, 6]) * inv_sin
    theta_imag = (cos_cycle * legendre_sums[:, 5] - legendre_sums[:, 7]) * inv_sin
    phi_real = -ratio * legendre_sums[:, 3] * inv_sin
    phi_imag = ratio * legendre_sums[:, 2] * inv_sin
    weight = (jnp.where(orders_int == 0, 1.0, 2.0) * mode_count ** (-0.5))[:, None]
    stacked = jnp.stack(
        [legendre_sums[:, 0], legendre_sums[:, 1], theta_real, theta_imag, phi_real, phi_imag],
        axis=1,
    )
    return (stacked * weight).astype(jnp.bfloat16)


def analysis_sets(spectra, colatitude, cycle_weight):
    with_cos = cycle_weight * jnp.cos(colatitude) / jnp.sin(colatitude)
    with_sin = cycle_weight / jnp.sin(colatitude)
    stacked = jnp.stack(
        [
            spectra[:, 0] * with_cos,
            spectra[:, 0] * with_sin,
            spectra[:, 1] * with_cos,
            spectra[:, 1] * with_sin,
        ],
        axis=1,
    )
    return stacked.reshape(spectra.shape[0], 8, spectra.shape[3], spectra.shape[4]).astype(
        jnp.bfloat16
    )


def estimate(merged, degree, orders, raising_factor, mode_count, cycle_count):
    level = degree[:, None, :]
    azimuth = orders[:, None, :]
    factor = raising_factor[:, None, :]

    def previous(values):
        return jnp.concatenate([jnp.zeros_like(values[..., :1]), values[..., :-1]], axis=-1)

    grad_real = (
        level * merged[:, :, 0] - factor * previous(merged[:, :, 2]) + azimuth * merged[:, :, 7]
    )
    grad_imag = (
        level * merged[:, :, 1] - factor * previous(merged[:, :, 3]) - azimuth * merged[:, :, 6]
    )
    curl_real = (
        level * merged[:, :, 4] - factor * previous(merged[:, :, 6]) - azimuth * merged[:, :, 3]
    )
    curl_imag = (
        level * merged[:, :, 5] - factor * previous(merged[:, :, 7]) + azimuth * merged[:, :, 2]
    )
    scale = (mode_count / cycle_count) ** 0.5 / jnp.sqrt(jnp.maximum(level * (level + 1.0), 1.0))
    scale = scale[:, :, None, :]
    return (
        jnp.stack([grad_real, grad_imag], axis=2) * scale,
        jnp.stack([curl_real, curl_imag], axis=2) * scale,
    )


def shards(tbar_alm, twf_alm, legendre, m_slots, cycle_order, colatitude, cycle_weight, pixel_mask):
    pairs_dev = tbar_alm.shape[0]
    row_count = tbar_alm.shape[3]
    mode_count = row_count - 1
    cycle_count = legendre.shape[2]
    cycle_dev = pixel_mask.shape[0]
    pixel_count = pixel_mask.shape[1]
    device_slot = lax.axis_index("ma")
    local_small = lax.dynamic_slice_in_dim(m_slots, device_slot * pairs_dev, pairs_dev)
    upper_half, degree, orders = pair_layout(local_small, mode_count)
    raising_factor = raising(degree, orders)
    coeff_sets = synthesis_sets(tbar_alm, twf_alm, degree, raising_factor, mode_count)
    halves = jnp.stack([jnp.logical_not(upper_half), upper_half], axis=1)
    masked = coeff_sets[:, None] * halves.astype(jnp.bfloat16)[:, :, None, None, :]
    legendre_sums = jnp.einsum(
        "phsck,pkr->scphr", masked, legendre, preferred_element_type=jnp.float32
    )
    legendre_sums = jnp.take(legendre_sums, cycle_order, axis=4)
    legendre_sums = legendre_sums.reshape(legendre_sums.shape[0], 8, 2 * pairs_dev, cycle_count)
    all_orders = mode_columns(m_slots, mode_count)
    dft_table = fourier_table(all_orders, pixel_count)
    pixel_weights = pixel_mask.astype(jnp.float32)
    slot_theta = jnp.take(colatitude, cycle_order)
    local_orders = mode_columns(local_small, mode_count)
    outgoing = combine_modes(
        legendre_sums, local_orders, jnp.cos(slot_theta), jnp.sin(slot_theta), mode_count
    )
    fourier = lax.all_to_all(outgoing, "ma", split_axis=3, concat_axis=2, tiled=True)
    fourier = fourier.reshape(fourier.shape[0], 3, 2, mode_count, cycle_dev)
    cycle_maps = jnp.einsum(
        "sqemr,emj->sqrj", fourier, dft_table, preferred_element_type=jnp.float32
    )
    products = (pixel_weights * cycle_maps[:, 0:1] * cycle_maps[:, 1:3]).astype(jnp.bfloat16)
    spectra = jnp.einsum("sqrj,emj->sqemr", products, dft_table, preferred_element_type=jnp.float32)
    received = (spectra * pixel_count ** (-0.5)).astype(jnp.bfloat16)
    returned = lax.all_to_all(received, "ma", split_axis=3, concat_axis=4, tiled=True)
    inverse = (
        jnp.zeros((cycle_count,), jnp.int32).at[cycle_order].set(lax.iota(jnp.int32, cycle_count))
    )
    spectra = jnp.take(returned, inverse, axis=4).astype(jnp.float32)
    weighted = analysis_sets(spectra, colatitude, cycle_weight)
    weighted = weighted.reshape(weighted.shape[0], 8, pairs_dev, 2, cycle_count)
    projected = jnp.einsum(
        "scphr,pkr->phsck", weighted, legendre, preferred_element_type=jnp.float32
    )
    merged = jnp.sum(projected * halves.astype(jnp.float32)[:, :, None, None, :], axis=1)
    return estimate(merged, degree, orders, raising_factor, mode_count, cycle_count)


def solution(mesh):
    return jax.shard_map(
        shards,
        mesh=mesh,
        in_specs=(
            P("ma", "grp", None, None),
            P("ma", "grp", None, None),
            P("ma", None, None),
            P(),
            P(),
            P(),
            P(),
            P("ma", None),
        ),
        out_specs=(P("ma", "grp", None, None), P("ma", "grp", None, None)),
        check_vma=False,
    )
```

profile of v0, /device:TPU:0, one launch (start us, length us, event | category | flops | bytes accessed | tf_op | source)
XLA Modules:
  0.0 57.9 jit_solution(10242634257590301052)
XLA Ops:
  0.7 0.8 %fusion.67 = (s32[8,1]{0,1:T(1,128)S(1)}, s32[8]{0:T(128)S(1)}) fusion(s32[128]{0:T(128)} %param.11, s32[]{:T(128)S(6)} %select_n.118), kind=kLoop, calls=%fused_computation.132 | loop fusion | flops 8 | bytes 100 | tf_op jit(solution)/shard_map/stack | solution.py:46
  1.7 0.8 %copy_bitcast_fusion.8 = (bf16[8,4,1,2,257]{4,0,3,2,1:T(8,128)(2,1)S(1)}, f32[8,4,2,257]{3,0,2,1:T(8,128)S(1)}) fusion(bf16[8,4,2,257]{3,2,1,0:T(2,128)(2,1)} %param.9), kind=kLoop, calls=%fused_computation.81 | loop fusion | flops 16448 | bytes 131584 | tf_op jit(solution)/shard_map/stack | solution.py:31
  2.5 0.8 %fusion.31 = bf16[8,4,1,2,257]{4,0,3,2,1:T(8,128)(2,1)S(1)} fusion(f32[8,257]{1,0:T(8,128)S(1)} %get-tuple-element.43, bf16[8,4,2,257]{3,2,1,0:T(2,128)(2,1)} %param.9), kind=kLoop, calls=%fused_computation.53 | loop fusion | flops 49344 | bytes 74016 | tf_op jit(solution)/shard_map/stack | solution.py:31
  3.5 0.8 %copy_bitcast_fusion.7 = (bf16[8,4,1,2,257]{4,0,3,2,1:T(8,128)(2,1)S(1)}, bf16[8,4,1,2,257]{4,0,3,2,1:T(8,128)(2,1)S(1)}) fusion(bf16[8,4,2,257]{3,2,1,0:T(2,128)(2,1)} %param.8, bf16[8,4,2,256]{3,0,2,1:T(8,128)(2,1)S(1)} %fusion.29), kind=kLoop, calls=%fused_computation.77 | loop fusion | bytes 131456 | tf_op jit(solution)/shard_map/stack | solution.py:31
  4.4 0.2 convolution_bitcast_fusion.1
  4.7 0.3 copy.109
  5.0 0.6 %scatter_custom_fusion = s32[16]{0:T(128)S(1)} fusion(s32[16]{0:T(128)S(1)} %compare_select_fusion.1, s32[16]{0:T(128)S(1)} %iota.74, s32[]{:T(128)} %constant.42.clone.1), kind=kCustom, calls=%fused_computation.126 | custom fusion | bytes 68 | tf_op jit(solution)/shard_map/scatter | solution.py:154
  5.6 0.6 %gather_fusion = f32[16,4,8,8,2]{3,2,4,1,0:T(8,128)S(1)} fusion(f32[4,8,8,2,16]{2,1,4,3,0:T(8,128)S(1)} %copy.109, s32[1024]{0:T(1024)S(1)} %get-tuple-element.59), kind=kCustom, calls=%fused_computation | custom fusion | bytes 65600 | tf_op jit(solution)/shard_map/jit(_take)/gather | solution.py:134
  6.3 0.3 copy.110
  6.6 0.7 %gather_fusion.1 = f32[16]{0:T(128)S(1)} fusion(f32[16]{0:T(128)S(1)} %copy-done.1, s32[1024]{0:T(1024)S(1)} %get-tuple-element.59), kind=kCustom, calls=%fused_computation.1 | custom fusion | bytes 192 | tf_op jit(solution)/shard_map/jit(_take)/gather | solution.py:139
  8.1 0.1 copy.114
  8.2 0.7 %reshape.622 = bf16[16,2,192]{2,1,0:T(2,128)(2,1)} reshape(bf16[16,6,4,16]{3,2,1,0:T(4,128)(2,1)S(1)} %bitcast.149) | data formatting | bytes 24576
  9.0 7.4 %all-to-all-start = ((bf16[16,2,192]{2,1,0:T(2,128)(2,1)}), bf16[16,2,192]{2,1,0:T(2,128)(2,1)S(1)}, u32[]{:S(2)}, u32[]{:S(2)}) async-start(bf16[16,2,192]{2,1,0:T(2,128)(2,1)} %reshape.622), calls=%async_computation | async-start | bytes 32768 | tf_op jit(solution)/shard_map/all_to_all | solution.py:144
  16.6 0.1 mul.372
  16.8 18.8 %cosine_convert_fusion = (bf16[1,256,4096]{2,1,0:T(8,128)(2,1)S(1)}, bf16[1,256,4096]{2,1,0:T(8,128)(2,1)}) fusion(s32[256]{0:T(256)S(1)} %mul.372), kind=kLoop, calls=%fused_computation.16 | loop fusion | flops 17825792 | bytes 4195328 | tf_op jit(solution)/shard_map/convert.15
  35.7 0.1 reshape.623
  35.9 0.1 reshape.578
  36.0 2.5 %convolution_bitcast_fusion = f32[4,3,1,4096]{3,0,1,2:T(4,128)S(1)} fusion(bf16[4,3,2,256]{3,0,2,1:T(4,128)(2,1)S(1)} %reshape.578, bf16[1,256,4096]{2,1,0:T(8,128)(2,1)} %get-tuple-element.51, bf16[1,256,4096]{2,1,0:T(8,128)(2,1)S(1)} %get-tuple-element.50), kind=kOutput, calls=%fused_computation.7 | convolution fusion | flops 52428800 | bytes 4403200 | tf_op jit(solution)/shard_map/sqemr,emj->sqrj/dot_general | solution.py:146
  38.6 1.2 %fusion.16 = bf16[4,2,2,256,1]{3,0,1,2,4:T(4,128)(2,1)S(1)} fusion(bf16[1,256,4096]{2,1,0:T(8,128)(2,1)S(1)} %copy-done.2, bf16[1,256,4096]{2,1,0:T(8,128)(2,1)S(1)} %get-tuple-element.50, f32[4,3,1,4096]{3,0,1,2:T(4,128)S(1)} %convolution_bitcast_fusion, f32[4,4096]{1,0:T(4,128)S(1)} %fusion.28), kind=kOutput, calls=%fused_computation.25 | convolution fusion | flops 42016768 | bytes 4399104 | tf_op jit(solution)/shard_map/sqrj,emj->sqemr/dot_general | solution.py:150
  39.7 0.2 copy.116
  40.0 0.9 %reshape.624 = bf16[16,2,128]{2,1,0:T(2,128)(2,1)} reshape(bf16[256,1,2,2,4]{4,3,2,1,0:T(2,128)(2,1)S(1)} %bitcast.146) | data formatting | bytes 16384
  40.9 6.0 %all-to-all-start.1 = ((bf16[16,2,128]{2,1,0:T(2,128)(2,1)}), bf16[16,2,128]{2,1,0:T(2,128)(2,1)S(1)}, u32[]{:S(2)}, u32[]{:S(2)}) async-start(bf16[16,2,128]{2,1,0:T(2,128)(2,1)} %reshape.624), calls=%async_computation.1 | async-start | bytes 16384 | tf_op jit(solution)/shard_map/all_to_all | solution.py:152
  46.9 6.3 %all-to-all-done.1 = bf16[16,2,128]{2,1,0:T(2,128)(2,1)S(1)} async-done(((bf16[16,2,128]{2,1,0:T(2,128)(2,1)}), bf16[16,2,128]{2,1,0:T(2,128)(2,1)S(1)}, u32[]{:S(2)}, u32[]{:S(2)}) %all-to-all-start.1) | async-done | bytes 8224 | tf_op jit(solution)/shard_map/all_to_all | solution.py:152
  53.3 0.6 reshape.625
  53.9 0.5 copy.118
  54.3 0.7 %gather_fusion.2 = bf16[16,4,2,2,16]{4,1,3,2,0:T(4,128)(2,1)S(1)} fusion(bf16[4,2,2,16,16]{3,0,4,2,1:T(4,128)(2,1)S(1)} %bitcast.150, s32[1024]{0:T(1024)S(1)} %get-tuple-element.58), kind=kCustom, calls=%fused_computation.2 | custom fusion | bytes 16448 | tf_op jit(solution)/shard_map/jit(_take)/gather | solution.py:156
  55.3 0.2 copy.119
  55.5 0.2 fusion.9
  55.8 0.3 fusion.71
  56.2 0.2 fusion.35
  56.5 0.7 %copy.130 = f32[8,4,2,257]{3,2,1,0:T(2,128)} copy(f32[8,4,2,257]{3,1,0,2:T(4,128)S(1)} %get-tuple-element.39) | data formatting | bytes 131584
  57.2 0.7 %copy.131 = f32[8,4,2,257]{3,2,1,0:T(2,128)} copy(f32[8,4,2,257]{3,1,0,2:T(4,128)S(1)} %get-tuple-element.38) | data formatting | bytes 131584
  (65 shorter events, 2.1 us)
Async XLA Ops:
  0.6 3.8 %copy-start = (bf16[8,257,16]{1,2,0:T(8,128)(2,1)S(1)}, bf16[8,257,16]{1,2,0:T(8,128)(2,1)}, u32[]{:S(2)}) copy-start(bf16[8,257,16]{1,2,0:T(8,128)(2,1)} %param.10) | copy-start | bytes 197380
  0.6 4.3 %copy-start.5 = (s32[16]{0:T(128)S(1)}, s32[16]{0:T(128)}, u32[]{:S(2)}) copy-start(s32[16]{0:T(128)} %param.12) | copy-start | bytes 196
  1.7 4.9 %copy-start.1 = (f32[16]{0:T(128)S(1)}, f32[16]{0:T(128)}, u32[]{:S(2)}) copy-start(f32[16]{0:T(128)} %param.13) | copy-start | bytes 196
  4.7 11.7 %copy-start.4 = (s32[128]{0:T(128)S(1)}, s32[128]{0:T(128)}, u32[]{:S(2)}) copy-start(s32[128]{0:T(128)} %param.11) | copy-start | bytes 1540
  9.0 26.7 %all-to-all-start = ((bf16[16,2,192]{2,1,0:T(2,128)(2,1)}), bf16[16,2,192]{2,1,0:T(2,128)(2,1)S(1)}, u32[]{:S(2)}, u32[]{:S(2)}) async-start(bf16[16,2,192]{2,1,0:T(2,128)(2,1)} %reshape.622), calls=%async_computation | async-start | bytes 32768 | tf_op jit(solution)/shard_map/all_to_all | solution.py:144
  16.7 18.9 %copy-start.6 = (f32[16]{0:T(128)S(1)}, f32[16]{0:T(128)}, u32[]{:S(2)}) copy-start(f32[16]{0:T(128)} %param.14) | copy-start | bytes 196
  16.8 18.9 %copy-start.3 = (s32[1,4096]{1,0:T(1,128)S(1)}, s32[1,4096]{1,0:T(1,128)}, u32[]{:S(2)}) copy-start(s32[1,4096]{1,0:T(1,128)} %param.15) | copy-start | bytes 49156
  36.0 2.5 %copy-start.2 = (bf16[1,256,4096]{2,1,0:T(8,128)(2,1)S(1)}, bf16[1,256,4096]{2,1,0:T(8,128)(2,1)}, u32[]{:S(2)}) copy-start(bf16[1,256,4096]{2,1,0:T(8,128)(2,1)} %get-tuple-element.51) | copy-start | bytes 6291460
  40.9 12.4 %all-to-all-start.1 = ((bf16[16,2,128]{2,1,0:T(2,128)(2,1)}), bf16[16,2,128]{2,1,0:T(2,128)(2,1)S(1)}, u32[]{:S(2)}, u32[]{:S(2)}) async-start(bf16[16,2,128]{2,1,0:T(2,128)(2,1)} %reshape.624), calls=%async_computation.1 | async-start | bytes 16384 | tf_op jit(solution)/shard_map/all_to_all | solution.py:152
where the time goes:
time: 58.3 us; the launch traced here: 57.9 us
  other arithmetic  22.9 us (39%)
  starting transfers between devices  13.4 us (23%)
  local copies, waits for them, and re-layouts  10 us (17%)
  waiting for transfers between devices  6.35 us (11%)
  matrix products  4.14 us (7%)
  between operations  1.12 us (2%)
    another operation x3, other arithmetic  19 us
    all_to_all x1, starting transfers between devices, shards(): lax.all_to_all(outgoing, 'ma', split_axis=3, concat_axis=2, tiled=True)  7.41 us
    all_to_all x1, waiting for transfers between devices, shards(): lax.all_to_all(received, 'ma', split_axis=3, concat_axis=4, tiled=True)  6.35 us
    all_to_all x1, starting transfers between devices, shards(): lax.all_to_all(received, 'ma', split_axis=3, concat_axis=4, tiled=True)  6.01 us
    unnamed x25, local copies, waits for them, and re-layouts  3.89 us
    dot_general x1, matrix products, shards(): jnp.einsum('sqemr,emj->sqrj', fourier, dft_table, preferred_element_type=...  2.47 us
    another operation x3, other arithmetic, synthesis_sets(): jnp.stack([tbar_alm.astype(jnp.float32), wiener, (degree / mode_count)[:,...  1.69 us
    dot_general x1, matrix products, shards(): jnp.einsum('sqrj,emj->sqemr', products, dft_table, preferred_element_type...  1.19 us
  transfers between devices with their start and end apart: 2, of which 1 were waited for; matrix products, arithmetic and copies ran while one was open for 33% of the time, Pallas kernels for 0%

commit v1 on v0

--- a/solution.py
+++ b/solution.py
@@ -1,8 +1,13 @@
 import math
+
+import functools
 
 import jax
 import jax.numpy as jnp
+import numpy as np
 from jax import lax
+from jax.experimental import pallas as pl
+from jax.experimental.pallas import tpu as pltpu
 from jax.sharding import PartitionSpec as P
 
 
@@ -163,9 +168,323 @@
     return estimate(merged, degree, orders, raising_factor, mode_count, cycle_count)
 
 
+LANES = 128
+F32 = jnp.float32
+BF16 = jnp.bfloat16
+
+
+def split_tables(mode_count, pixel_count, sims):
+    m = np.arange(mode_count)[None, :]
+    low = np.arange(LANES)[:, None]
+    high = np.repeat(np.arange(pixel_count // LANES), sims)[:, None] * LANES
+    fine = (m * low % pixel_count) * (2.0 * math.pi / pixel_count)
+    coarse = (m * high % pixel_count) * (2.0 * math.pi / pixel_count)
+    cos_high = np.cos(coarse).astype(np.float32)
+    sin_high = np.sin(coarse).astype(np.float32)
+
+    def halves(values):
+        upper = values.astype(BF16)
+        return upper, (values - upper.astype(np.float32)).astype(BF16)
+
+    return np.concatenate(
+        [np.cos(fine).astype(BF16), (-np.sin(fine)).astype(BF16)]
+        + list(halves(cos_high))
+        + list(halves(sin_high)),
+        axis=0,
+    )
+
+
+def iota(shape, axis):
+    return lax.broadcasted_iota(jnp.int32, shape, axis)
+
+
+def one_hot(condition):
+    return jnp.where(condition, 1.0, 0.0).astype(BF16)
+
+
+def dot(left, right):
+    return jnp.dot(left, right, preferred_element_type=F32)
+
+
+def dot_t(left, right):
+    return lax.dot_general(left, right, (((1,), (1,)), ((), ())), preferred_element_type=F32)
+
+
+def fused_kernel(
+    n, modes, rows, cycles, pixels, sims,
+    slots_s, cycle_s, colat_s, weight_s, slots_v, tbar_ref, twf_ref, leg_ref, prev_ref, mask_ref,
+    table_hbm, grad_ref, curl_ref,
+    table_v, leg_all, prev_all, send_f, recv_f, send_p, recv_p,
+    table_sem, fs_sem, fr_sem, ps_sem, pr_sem,
+):
+    me = lax.axis_index("ma")
+    pairs, padded = tbar_ref.shape[0], tbar_ref.shape[2]
+    block = 2 * pairs
+    comps = 2 * sims
+    span = 2 * cycles
+    total = pairs * span
+    fetch = pltpu.make_async_copy(table_hbm, table_v, table_sem)
+    fetch.start()
+    barrier = pltpu.get_barrier_semaphore()
+    for off in range(1, n):
+        pl.semaphore_signal(
+            barrier, inc=1, device_id={"ma": lax.rem(me + off, n)},
+            device_id_type=pl.DeviceIdType.MESH,
+        )
+
+    row_shape = (pairs, padded)
+    smaller = jnp.zeros(row_shape, jnp.int32)
+    for p in range(pairs):
+        smaller = jnp.where(iota(row_shape, 0) == p, slots_s[me * pairs + p], smaller)
+    k = iota(row_shape, 1)
+    upper = k >= modes - smaller
+    degree = jnp.where(upper, k - 1, smaller + k).astype(F32)
+    orders = jnp.where(upper, modes - 1 - smaller, smaller).astype(F32)
+    eps = raising(degree, orders)
+    upper_f = jnp.where(upper, 1.0, 0.0)
+    lower_f = 1.0 - upper_f
+
+    colat = jnp.zeros((cycles, 4 * comps), F32)
+    for r in range(cycles):
+        colat = jnp.where(iota(colat.shape, 0) == r, colat_s[r], colat)
+    csc = 1.0 / jnp.sin(colat)
+    cot = jnp.cos(colat) * csc
+    lane = iota(colat.shape, 1)
+    group = lane // comps
+    part_a = jnp.where(group == 0, 1.0, jnp.where(group == 1, cot, 0.0))
+    part_m = jnp.where(group == 2, csc, 0.0)
+    part_b = jnp.where(group == 1, csc, 0.0)
+
+    blank = jnp.zeros((comps, padded), F32)
+    pieces = []
+    for p in range(pairs):
+        twf = twf_ref[p].astype(F32)
+        deg_p, eps_p = degree[p : p + 1] / modes, eps[p : p + 1] / modes
+        sets_a = jnp.concatenate([tbar_ref[p].astype(F32), deg_p * twf, twf, blank], axis=0)
+        sets_b = jnp.concatenate([blank, -(eps_p * twf), blank, blank], axis=0)
+        leg, prev = leg_ref[p].astype(F32), prev_ref[p].astype(F32)
+        low, high = lower_f[p : p + 1], upper_f[p : p + 1]
+        leg = jnp.concatenate([leg * low, leg * high], axis=0).astype(BF16)
+        prev = jnp.concatenate([prev * low, prev * high], axis=0).astype(BF16)
+        leg_all[pl.ds(p * span, span), :] = leg
+        prev_all[pl.ds(p * span, span), :] = prev
+        out_a = dot_t(leg, sets_a.astype(BF16))
+        out_b = dot_t(prev, sets_b.astype(BF16))
+        for h in range(2):
+            small = slots_s[me * pairs + p]
+            order = modes - 1 - small if h else small
+            norm = jnp.where(order == 0, 1.0, 2.0) * modes ** (-0.5)
+            ratio = order.astype(F32) / modes
+            rng = slice(h * cycles, (h + 1) * cycles)
+            pieces.append((out_a[rng] * (part_a + part_m * ratio) + out_b[rng] * part_b) * norm)
+    fourier = jnp.concatenate(pieces, axis=0).astype(BF16)
+
+    base_shape = (block, total)
+    row = iota(base_shape, 0)
+    base = iota(base_shape, 1) - (lax.rem(row, pairs) * span + (row // pairs) * cycles)
+    place = jnp.concatenate(
+        [jnp.where(base == cycle_s[i], 1.0, 0.0) for i in range(cycles)], axis=0
+    ).astype(BF16)
+    placed = dot(place, fourier).astype(BF16)
+    send_f[:, :, : 4 * comps] = placed.reshape(n, block, 4 * comps)
+
+    def exchange(send, recv, s_sem, r_sem):
+        copies = []
+        for off in range(1, n):
+            to = lax.rem(me + off, n)
+            copy = pltpu.make_async_remote_copy(
+                src_ref=send.at[to], dst_ref=recv.at[me], send_sem=s_sem.at[off],
+                recv_sem=r_sem.at[off], device_id={"ma": to},
+                device_id_type=pl.DeviceIdType.MESH,
+            )
+            copy.start()
+            copies.append(copy)
+        recv[me] = send[me]
+        return copies
+
+    pl.semaphore_wait(barrier, n - 1)
+    copies = exchange(send_f, recv_f, fs_sem, fr_sem)
+
+    spread_shape = (slots_v.shape[1], n * block)
+    col = iota(spread_shape, 1)
+    spread = one_hot(
+        iota(spread_shape, 0) == (col // block) * pairs + lax.rem(col, pairs)
+    )
+    slots = jnp.broadcast_to(slots_v[...], (8, slots_v.shape[1]))
+    high_part = (slots // 256).astype(F32)
+    low_part = lax.rem(slots, 256).astype(F32)
+    picked = 256.0 * dot(high_part.astype(BF16), spread) + dot(low_part.astype(BF16), spread)
+    flip = lax.rem(iota(picked.shape, 1), block) >= pairs
+    picked = jnp.where(flip, modes - 1.0 - picked, picked)[0:1]
+    select = one_hot(iota((modes, n * block), 0).astype(F32) == picked)
+
+    hs = pixels // LANES * sims
+    fetch.wait()
+    moved = dot(table_v[...], select)
+    fine_cos, fine_sin = moved[:LANES], moved[LANES : 2 * LANES]
+    at = 2 * LANES
+    cos_t = moved[at : at + hs] + moved[at + hs : at + 2 * hs]
+    sin_t = moved[at + 2 * hs : at + 3 * hs] + moved[at + 3 * hs : at + 4 * hs]
+    cos_h, sin_h = cos_t.T, sin_t.T
+    synth = jnp.concatenate([fine_cos, fine_sin], axis=1).astype(BF16)
+    anal = jnp.concatenate([fine_cos.T, fine_sin.T], axis=0).astype(BF16)
+
+    exp_shape = (4 * comps, 6 * hs)
+    ecol = iota(exp_shape, 1)
+    which = ecol // hs
+    comp_q, comp_c = which // 2, lax.rem(which, 2)
+    source_c = jnp.where(comp_q == 2, 1 - comp_c, comp_c)
+    hit = iota(exp_shape, 0) == comp_q * comps + 2 * lax.rem(ecol, sims) + source_c
+    sign = jnp.where(jnp.logical_and(comp_q == 2, comp_c == 0), -1.0, 1.0)
+    expand = jnp.where(hit, sign, 0.0).astype(BF16)
+
+    sel_shape = (4 * hs, 4 * comps)
+    srow, scol = iota(sel_shape, 0), iota(sel_shape, 1)
+    row_q, row_c = srow // (2 * hs), lax.rem(srow // hs, 2)
+    out_g, out_c = scol // comps, lax.rem(scol, 2)
+    want_q = jnp.where(jnp.logical_or(out_g == 1, out_g == 2), 1, 0)
+    swap = out_g >= 2
+    want_c = jnp.where(swap, 1 - out_c, out_c)
+    same_s = lax.rem(srow, sims) == lax.rem(scol, comps) // 2
+    negative = jnp.logical_or(
+        jnp.logical_and(out_g == 2, out_c == 1), jnp.logical_and(out_g == 3, out_c == 0)
+    )
+    hit = jnp.logical_and(jnp.logical_and(row_q == want_q, row_c == want_c), same_s)
+    gather = jnp.where(hit, jnp.where(negative, -1.0, 1.0), 0.0).astype(BF16)
+
+    mask_t = mask_ref[...].astype(F32).T.astype(BF16)
+    m_shape = (pixels // LANES, hs)
+    mask = dot(mask_t, one_hot(iota(m_shape, 0) == iota(m_shape, 1) // sims))
+
+    lane_shape = (8, total)
+    cyc = lax.rem(iota(lane_shape, 1), cycles)
+    theta_l = jnp.zeros(lane_shape, F32)
+    weight_l = jnp.zeros(lane_shape, F32)
+    for r in range(cycles):
+        theta_l = jnp.where(cyc == r, colat_s[r], theta_l)
+        weight_l = jnp.where(cyc == r, weight_s[r], weight_l)
+    with_sin = (weight_l / jnp.sin(theta_l))[0:1]
+    with_cos = (weight_l * jnp.cos(theta_l) / jnp.sin(theta_l))[0:1]
+
+    for copy in copies:
+        copy.wait_recv()
+    got = recv_f[...].reshape(n * block, LANES)[:, : 4 * comps]
+    spread_f = dot(got, expand)
+    real, imag = [], []
+    for q in range(3):
+        re = spread_f[:, 2 * q * hs : (2 * q + 1) * hs]
+        im = spread_f[:, (2 * q + 1) * hs : (2 * q + 2) * hs]
+        real.append((re * cos_h - im * sin_h).astype(BF16))
+        imag.append((re * sin_h + im * cos_h).astype(BF16))
+    turned = jnp.concatenate(
+        [jnp.concatenate(real, axis=1), jnp.concatenate(imag, axis=1)], axis=0
+    )
+    maps = dot(synth, turned)
+    lead = mask * maps[:, :hs]
+    products = jnp.concatenate(
+        [lead * maps[:, hs : 2 * hs], lead * maps[:, 2 * hs :]], axis=1
+    ).astype(BF16)
+    half = dot(anal, products)
+    parts = []
+    count = n * block
+    for q in range(2):
+        c_part = half[:count, q * hs : (q + 1) * hs]
+        s_part = half[count:, q * hs : (q + 1) * hs]
+        parts.append((cos_h * c_part + sin_h * s_part).astype(BF16))
+        parts.append((cos_h * s_part - sin_h * c_part).astype(BF16))
+    spectra = dot(jnp.concatenate(parts, axis=1), gather) * pixels ** (-0.5)
+    send_p[:, :, : 4 * comps] = spectra.astype(BF16).reshape(n, block, 4 * comps)
+    back = exchange(send_p, recv_p, ps_sem, pr_sem)
+    scale = (modes / cycles) ** 0.5 / jnp.sqrt(jnp.maximum(degree * (degree + 1.0), 1.0))
+    f_level, f_eps, f_order = degree * scale, eps * scale, orders * scale
+    for copy in back:
+        copy.wait_recv()
+
+    came = recv_p[...].reshape(n * block, LANES)[:, : 4 * comps].astype(F32).T.astype(BF16)
+    by_pair = dot(came, place)
+    first = jnp.concatenate([by_pair[: 2 * comps] * with_cos, by_pair[2 * comps :] * with_sin], 0)
+    second = by_pair[: 2 * comps] * with_sin
+    owner = iota((1, total), 1) // span
+    keep = [jnp.where(owner == p, 1.0, 0.0) for p in range(pairs)]
+    first = jnp.concatenate([(first * keep[p]).astype(BF16) for p in range(pairs)], axis=0)
+    second = jnp.concatenate([(second * keep[p]).astype(BF16) for p in range(pairs)], axis=0)
+    here = dot(first, leg_all[...])
+    before = dot(second, prev_all[...])
+    for p in range(pairs):
+        a, b = 4 * comps * p, 2 * comps * p
+        lev, ep, az = f_level[p : p + 1], f_eps[p : p + 1], f_order[p : p + 1]
+        grad_ref[p] = (
+            lev * here[a : a + comps] - ep * before[b : b + comps]
+            + az * here[a + 2 * comps : a + 3 * comps]
+        )
+        curl_ref[p] = (
+            lev * here[a + comps : a + 2 * comps] - ep * before[b + comps : b + 2 * comps]
+            + az * here[a + 3 * comps : a + 4 * comps]
+        )
+    for copy in copies + back:
+        copy.wait_send()
+
+
+def fused(tbar_alm, twf_alm, legendre, m_slots, cycle_order, colatitude, cycle_weight, pixel_mask, n):
+    pairs, sims, _, rows = tbar_alm.shape
+    modes = rows - 1
+    cycles = legendre.shape[2]
+    pixels = pixel_mask.shape[1]
+    padded = -(-rows // LANES) * LANES
+    comps = 2 * sims
+    total = pairs * 2 * cycles
+    hs = pixels // LANES * sims
+    pad = ((0, 0), (0, 0), (0, padded - rows))
+    tbar = jnp.pad(tbar_alm.reshape(pairs, comps, rows), pad)
+    twf = jnp.pad(twf_alm.reshape(pairs, comps, rows), pad)
+    by_cycle = jnp.transpose(legendre, (0, 2, 1))
+    leg = jnp.pad(by_cycle, pad)
+    prev = jnp.pad(by_cycle[:, :, : rows - 1], ((0, 0), (0, 0), (1, padded - rows)))
+    table = jnp.asarray(split_tables(modes, pixels, sims))
+    vmem, smem = pl.BlockSpec(memory_space=pltpu.VMEM), pl.BlockSpec(memory_space=pltpu.SMEM)
+    out = jax.ShapeDtypeStruct((pairs, comps, padded), F32)
+    grad, curl = pl.pallas_call(
+        functools.partial(fused_kernel, n, modes, rows, cycles, pixels, sims),
+        out_shape=(out, out),
+        in_specs=[smem] * 4 + [vmem] * 6 + [pl.BlockSpec(memory_space=pl.ANY)],
+        out_specs=(vmem, vmem),
+        scratch_shapes=[
+            pltpu.VMEM(table.shape, BF16),
+            pltpu.VMEM((total, padded), BF16),
+            pltpu.VMEM((total, padded), BF16),
+        ]
+        + [pltpu.VMEM((n, 2 * pairs, LANES), BF16)] * 4
+        + [pltpu.SemaphoreType.DMA]
+        + [pltpu.SemaphoreType.DMA((n,))] * 4,
+        compiler_params=pltpu.CompilerParams(collective_id=0, has_side_effects=True),
+        name="estimator",
+    )(
+        m_slots, cycle_order, colatitude, cycle_weight, m_slots.reshape(1, -1), tbar, twf, leg,
+        prev, pixel_mask.reshape(pixels // LANES, LANES), table,
+    )
+    shape = (pairs, sims, 2, rows)
+    return grad[:, :, :rows].reshape(shape), curl[:, :, :rows].reshape(shape)
+
+
+def body(n, *args):
+    tbar_alm, legendre, pixel_mask = args[0], args[2], args[7]
+    pairs, sims, _, rows = tbar_alm.shape
+    cycles = legendre.shape[2]
+    fits = (
+        pairs == 8
+        and cycles % 16 == 0
+        and pixel_mask.shape[0] == 1
+        and pairs * 2 * cycles <= 512
+        and rows <= 1025
+        and (pixel_mask.shape[1] // LANES * sims) % LANES == 0
+        and sims % 4 == 0
+    )
+    return fused(*args, n) if fits else shards(*args)
+
+
 def solution(mesh):
     return jax.shard_map(
-        shards,
+        functools.partial(body, mesh.shape["ma"]),
         mesh=mesh,
         in_specs=(
             P("ma", "grp", None, None),

time: 58.3 us -> 25.4 us (0.44)
  other arithmetic: 22.9 us -> 0 us
  Pallas kernels: 0 us -> 18.2 us
  starting transfers between devices: 13.4 us -> 0 us
  waiting for transfers between devices: 6.35 us -> 0 us
  matrix products: 4.14 us -> 0 us
  local copies, waits for them, and re-layouts: 10 us -> 6.25 us
    another operation x12 -> x0, other arithmetic: 21.9 us -> none
    pallas_call x0 -> x1, Pallas kernels: none -> 18.2 us  [fused(): pl.pallas_call(functools.partial(fused_kernel, n, modes, rows, cycles, pi...]
    all_to_all x2 -> x0, starting transfers between devices: 13.4 us -> none  [the longest x1 7.41 us: shards(): lax.all_to_all(outgoing, 'ma', split_axis=3, concat_axis=2, tiled=True)]
    all_to_all x2 -> x0, waiting for transfers between devices: 6.35 us -> none  [the longest x1 6.35 us: shards(): lax.all_to_all(received, 'ma', split_axis=3, concat_axis=4, tiled=True)]
    dot_general x4 -> x0, matrix products: 4.14 us -> none  [the longest x1 2.47 us: shards(): jnp.einsum('sqemr,emj->sqrj', fourier, dft_table, preferred_element_type=...]
    unnamed x25 -> x6, local copies, waits for them, and re-layouts: 3.89 us -> 0.38 us
    reshape x0 -> x4, local copies, waits for them, and re-layouts: none -> 3.21 us  [the longest x2 2.32 us: fused(): return (grad[:, :, :rows].reshape(shape), curl[:, :, :rows].reshape(shape))]
    pad x0 -> x4, local copies, waits for them, and re-layouts: none -> 2.66 us  [the longest x1 0.74 us: fused(): jnp.pad(by_cycle[:, :, :rows - 1], ((0, 0), (0, 0), (1, padded - rows)))]
  transfers between devices with their start and end apart: 2 -> 0, of which waited for: 1 -> 0; matrix products, arithmetic and copies ran while one was open for 33% -> 0% of each run, Pallas kernels for 0% -> 0%
where the time goes in v1:
time: 25.4 us; the launch traced here: 25.1 us
  Pallas kernels  18.2 us (72%)
  local copies, waits for them, and re-layouts  6.25 us (25%)
  between operations  0.66 us (3%)
    pallas_call x1, Pallas kernels, fused(): pl.pallas_call(functools.partial(fused_kernel, n, modes, rows, cycles, pi...  18.2 us
    reshape x2, local copies, waits for them, and re-layouts, fused(): return (grad[:, :, :rows].reshape(shape), curl[:, :, :rows].reshape(shape))  2.32 us
    reshape x1, local copies, waits for them, and re-layouts, fused(): tbar = jnp.pad(tbar_alm.reshape(pairs, comps, rows), pad)  0.84 us
    pad x1, local copies, waits for them, and re-layouts, fused(): jnp.pad(by_cycle[:, :, :rows - 1], ((0, 0), (0, 0), (1, padded - rows)))  0.74 us
    pad x1, local copies, waits for them, and re-layouts, fused(): leg = jnp.pad(by_cycle, pad)  0.65 us
    pad x1, local copies, waits for them, and re-layouts, fused(): twf = jnp.pad(twf_alm.reshape(pairs, comps, rows), pad)  0.64 us
    pad x1, local copies, waits for them, and re-layouts, fused(): tbar = jnp.pad(tbar_alm.reshape(pairs, comps, rows), pad)  0.63 us

profile of v1, /device:TPU:0, one launch (start us, length us, event | category | flops | bytes accessed | tf_op | source)
XLA Modules:
  0.0 25.1 jit_solution(12748301759993199615)
XLA Ops:
  0.6 0.8 %reshape.23 = bf16[8,8,257]{2,1,0:T(8,128)(2,1)S(1)} reshape(bf16[8,4,2,257]{3,2,1,0:T(2,128)(2,1)} %param.9) | data formatting | bytes 65792 | tf_op jit(solution)/shard_map/reshape | solution.py:438
  1.5 0.0 copy-start.2
  1.5 0.6 %pad.15.tbar_ref = bf16[8,8,384]{2,1,0:T(8,128)(2,1)} pad(bf16[8,8,257]{2,1,0:T(8,128)(2,1)S(1)} %reshape.23, bf16[]{:T(256)} %constant.4.clone.1), padding=0_0x0_0x0_127 | pad | bytes 82050 | tf_op jit(solution)/shard_map/jit(_pad)/pad | solution.py:438
  2.1 0.2 copy-done.2
  2.3 0.0 copy-start
  2.3 0.6 %pad.16.twf_ref = bf16[8,8,384]{2,1,0:T(8,128)(2,1)} pad(bf16[8,8,257]{2,1,0:T(8,128)(2,1)S(1)} %reshape.24, bf16[]{:T(256)} %constant.4.clone.1), padding=0_0x0_0x0_127 | pad | bytes 82050 | tf_op jit(solution)/shard_map/jit(_pad)/pad | solution.py:439
  3.0 0.2 copy-done
  3.2 0.7 %pad.18.prev_ref = bf16[8,16,384]{2,1,0:T(8,128)(2,1)} pad(bf16[8,16,256]{2,1,0:T(8,128)(2,1)S(1)} %slice.12, bf16[]{:T(256)} %constant.4.clone.1), padding=0_0x0_0x1_127 | pad | bytes 163842 | tf_op jit(solution)/shard_map/jit(_pad)/pad | solution.py:442
  3.9 0.7 %pad.17.leg_ref = bf16[8,16,384]{2,1,0:T(8,128)(2,1)} pad(bf16[8,16,257]{2,1,0:T(8,128)(2,1)S(1)} %bitcast.6, bf16[]{:T(256)} %constant.4.clone.1), padding=0_0x0_0x0_127 | pad | bytes 164098 | tf_op jit(solution)/shard_map/jit(_pad)/pad | solution.py:441
  4.6 18.2 %estimator.1 = (f32[8,8,384]{2,1,0:T(8,128)}, f32[8,8,384]{2,1,0:T(8,128)}) custom-call(s32[128]{0:T(128)} %slots_s.1, s32[16]{0:T(128)} %cycle_s.1, f32[16]{0:T(128)} %colat_s.1, f32[16]{0:T(128)} %weight_s.1, s32[1,128]{1,0:T(1,128)} %bitcast.10, bf16[8,8,384]{2,1,0:T(8,128)(2,1)} %pad.15.tbar_ref, bf16[8,8,384]{2,1,0:T(8,128)(2,1)} %pad.16.twf_ref, ...), custom_call_target="tpu_custom_call" | custom-call | tf_op jit(solution)/shard_map/estimator/pallas_call | solution.py:446
  22.7 0.0 copy-start.1
  22.7 1.6 %reshape.26 = f32[8,4,2,257]{3,2,1,0:T(2,128)} reshape(f32[8,8,257]{2,1,0:T(8,128)} %bitcast.8) | data formatting | bytes 131584 | tf_op jit(solution)/shard_map/reshape | solution.py:466
  24.4 0.0 copy-done.1
  24.4 0.7 %reshape.27 = f32[8,4,2,257]{3,2,1,0:T(2,128)} reshape(f32[8,8,257]{2,1,0:T(8,128)S(1)} %bitcast.7) | data formatting | bytes 131584 | tf_op jit(solution)/shard_map/reshape | solution.py:466
  (2 shorter events, 0.1 us)
Async XLA Ops:
  1.5 0.8 %copy-start.2 = (bf16[8,4,2,257]{3,2,1,0:T(2,128)(2,1)S(1)}, bf16[8,4,2,257]{3,2,1,0:T(2,128)(2,1)}, u32[]{:S(2)}) copy-start(bf16[8,4,2,257]{3,2,1,0:T(2,128)(2,1)} %param.10) | copy-start | bytes 98692
  2.3 0.9 %copy-start = (bf16[8,257,16]{1,2,0:T(8,128)(2,1)S(1)}, bf16[8,257,16]{1,2,0:T(8,128)(2,1)}, u32[]{:S(2)}) copy-start(bf16[8,257,16]{1,2,0:T(8,128)(2,1)} %param.11) | copy-start | bytes 197380
  22.7 1.6 %copy-start.1 = (f32[8,8,384]{2,1,0:T(8,128)S(1)}, f32[8,8,384]{2,1,0:T(8,128)}, u32[]{:S(2)}) copy-start(f32[8,8,384]{2,1,0:T(8,128)} %get-tuple-element.5) | copy-start | bytes 294916

commit v2 on v1

--- a/solution.py
+++ b/solution.py
@@ -198,6 +198,14 @@
     return lax.broadcasted_iota(jnp.int32, shape, axis)
 
 
+def div(values, size):
+    return values >> (size.bit_length() - 1)
+
+
+def mod(values, size):
+    return values & (size - 1)
+
+
 def one_hot(condition):
     return jnp.where(condition, 1.0, 0.0).astype(BF16)
 
@@ -212,13 +220,13 @@
 
 def fused_kernel(
     n, modes, rows, cycles, pixels, sims,
-    slots_s, cycle_s, colat_s, weight_s, slots_v, tbar_ref, twf_ref, leg_ref, prev_ref, mask_ref,
+    slots_s, cycle_s, colat_s, weight_s, slots_v, tbar_ref, twf_ref, leg_ref, mask_ref,
     table_hbm, grad_ref, curl_ref,
     table_v, leg_all, prev_all, send_f, recv_f, send_p, recv_p,
     table_sem, fs_sem, fr_sem, ps_sem, pr_sem,
 ):
     me = lax.axis_index("ma")
-    pairs, padded = tbar_ref.shape[0], tbar_ref.shape[2]
+    pairs, padded = tbar_ref.shape[0], rows
     block = 2 * pairs
     comps = 2 * sims
     span = 2 * cycles
@@ -250,7 +258,7 @@
     csc = 1.0 / jnp.sin(colat)
     cot = jnp.cos(colat) * csc
     lane = iota(colat.shape, 1)
-    group = lane // comps
+    group = div(lane, comps)
     part_a = jnp.where(group == 0, 1.0, jnp.where(group == 1, cot, 0.0))
     part_m = jnp.where(group == 2, csc, 0.0)
     part_b = jnp.where(group == 1, csc, 0.0)
@@ -258,11 +266,13 @@
     blank = jnp.zeros((comps, padded), F32)
     pieces = []
     for p in range(pairs):
-        twf = twf_ref[p].astype(F32)
+        tbar = jnp.concatenate([tbar_ref[p, s].astype(F32) for s in range(sims)], axis=0)
+        twf = jnp.concatenate([twf_ref[p, s].astype(F32) for s in range(sims)], axis=0)
         deg_p, eps_p = degree[p : p + 1] / modes, eps[p : p + 1] / modes
-        sets_a = jnp.concatenate([tbar_ref[p].astype(F32), deg_p * twf, twf, blank], axis=0)
+        sets_a = jnp.concatenate([tbar, deg_p * twf, twf, blank], axis=0)
         sets_b = jnp.concatenate([blank, -(eps_p * twf), blank, blank], axis=0)
-        leg, prev = leg_ref[p].astype(F32), prev_ref[p].astype(F32)
+        leg = leg_ref[p].astype(F32)
+        prev = jnp.concatenate([jnp.zeros_like(leg[:, :1]), leg[:, : rows - 1]], axis=1)
         low, high = lower_f[p : p + 1], upper_f[p : p + 1]
         leg = jnp.concatenate([leg * low, leg * high], axis=0).astype(BF16)
         prev = jnp.concatenate([prev * low, prev * high], axis=0).astype(BF16)
@@ -281,7 +291,7 @@
 
     base_shape = (block, total)
     row = iota(base_shape, 0)
-    base = iota(base_shape, 1) - (lax.rem(row, pairs) * span + (row // pairs) * cycles)
+    base = iota(base_shape, 1) - (mod(row, pairs) * span + div(row, pairs) * cycles)
     place = jnp.concatenate(
         [jnp.where(base == cycle_s[i], 1.0, 0.0) for i in range(cycles)], axis=0
     ).astype(BF16)
@@ -308,13 +318,13 @@
     spread_shape = (slots_v.shape[1], n * block)
     col = iota(spread_shape, 1)
     spread = one_hot(
-        iota(spread_shape, 0) == (col // block) * pairs + lax.rem(col, pairs)
+        iota(spread_shape, 0) == div(col, block) * pairs + mod(col, pairs)
     )
     slots = jnp.broadcast_to(slots_v[...], (8, slots_v.shape[1]))
-    high_part = (slots // 256).astype(F32)
-    low_part = lax.rem(slots, 256).astype(F32)
+    high_part = div(slots, 256).astype(F32)
+    low_part = mod(slots, 256).astype(F32)
     picked = 256.0 * dot(high_part.astype(BF16), spread) + dot(low_part.astype(BF16), spread)
-    flip = lax.rem(iota(picked.shape, 1), block) >= pairs
+    flip = mod(iota(picked.shape, 1), block) >= pairs
     picked = jnp.where(flip, modes - 1.0 - picked, picked)[0:1]
     select = one_hot(iota((modes, n * block), 0).astype(F32) == picked)
 
@@ -331,21 +341,21 @@
 
     exp_shape = (4 * comps, 6 * hs)
     ecol = iota(exp_shape, 1)
-    which = ecol // hs
-    comp_q, comp_c = which // 2, lax.rem(which, 2)
+    which = div(ecol, hs)
+    comp_q, comp_c = div(which, 2), mod(which, 2)
     source_c = jnp.where(comp_q == 2, 1 - comp_c, comp_c)
-    hit = iota(exp_shape, 0) == comp_q * comps + 2 * lax.rem(ecol, sims) + source_c
+    hit = iota(exp_shape, 0) == comp_q * comps + 2 * mod(ecol, sims) + source_c
     sign = jnp.where(jnp.logical_and(comp_q == 2, comp_c == 0), -1.0, 1.0)
     expand = jnp.where(hit, sign, 0.0).astype(BF16)
 
     sel_shape = (4 * hs, 4 * comps)
     srow, scol = iota(sel_shape, 0), iota(sel_shape, 1)
-    row_q, row_c = srow // (2 * hs), lax.rem(srow // hs, 2)
-    out_g, out_c = scol // comps, lax.rem(scol, 2)
+    row_q, row_c = div(srow, 2 * hs), mod(div(srow, hs), 2)
+    out_g, out_c = div(scol, comps), mod(scol, 2)
     want_q = jnp.where(jnp.logical_or(out_g == 1, out_g == 2), 1, 0)
     swap = out_g >= 2
     want_c = jnp.where(swap, 1 - out_c, out_c)
-    same_s = lax.rem(srow, sims) == lax.rem(scol, comps) // 2
+    same_s = mod(srow, sims) == div(mod(scol, comps), 2)
     negative = jnp.logical_or(
         jnp.logical_and(out_g == 2, out_c == 1), jnp.logical_and(out_g == 3, out_c == 0)
     )
@@ -354,10 +364,10 @@
 
     mask_t = mask_ref[...].astype(F32).T.astype(BF16)
     m_shape = (pixels // LANES, hs)
-    mask = dot(mask_t, one_hot(iota(m_shape, 0) == iota(m_shape, 1) // sims))
+    mask = dot(mask_t, one_hot(iota(m_shape, 0) == div(iota(m_shape, 1), sims)))
 
     lane_shape = (8, total)
-    cyc = lax.rem(iota(lane_shape, 1), cycles)
+    cyc = mod(iota(lane_shape, 1), cycles)
     theta_l = jnp.zeros(lane_shape, F32)
     weight_l = jnp.zeros(lane_shape, F32)
     for r in range(cycles):
@@ -404,7 +414,7 @@
     by_pair = dot(came, place)
     first = jnp.concatenate([by_pair[: 2 * comps] * with_cos, by_pair[2 * comps :] * with_sin], 0)
     second = by_pair[: 2 * comps] * with_sin
-    owner = iota((1, total), 1) // span
+    owner = div(iota((1, total), 1), span)
     keep = [jnp.where(owner == p, 1.0, 0.0) for p in range(pairs)]
     first = jnp.concatenate([(first * keep[p]).astype(BF16) for p in range(pairs)], axis=0)
     second = jnp.concatenate([(second * keep[p]).astype(BF16) for p in range(pairs)], axis=0)
@@ -413,14 +423,17 @@
     for p in range(pairs):
         a, b = 4 * comps * p, 2 * comps * p
         lev, ep, az = f_level[p : p + 1], f_eps[p : p + 1], f_order[p : p + 1]
-        grad_ref[p] = (
+        grad = (
             lev * here[a : a + comps] - ep * before[b : b + comps]
             + az * here[a + 2 * comps : a + 3 * comps]
         )
-        curl_ref[p] = (
+        curl = (
             lev * here[a + comps : a + 2 * comps] - ep * before[b + comps : b + 2 * comps]
             + az * here[a + 3 * comps : a + 4 * comps]
         )
+        for s in range(sims):
+            grad_ref[p, s] = grad[2 * s : 2 * s + 2]
+            curl_ref[p, s] = curl[2 * s : 2 * s + 2]
     for copy in copies + back:
         copy.wait_send()
 
@@ -430,28 +443,20 @@
     modes = rows - 1
     cycles = legendre.shape[2]
     pixels = pixel_mask.shape[1]
-    padded = -(-rows // LANES) * LANES
-    comps = 2 * sims
     total = pairs * 2 * cycles
-    hs = pixels // LANES * sims
-    pad = ((0, 0), (0, 0), (0, padded - rows))
-    tbar = jnp.pad(tbar_alm.reshape(pairs, comps, rows), pad)
-    twf = jnp.pad(twf_alm.reshape(pairs, comps, rows), pad)
     by_cycle = jnp.transpose(legendre, (0, 2, 1))
-    leg = jnp.pad(by_cycle, pad)
-    prev = jnp.pad(by_cycle[:, :, : rows - 1], ((0, 0), (0, 0), (1, padded - rows)))
     table = jnp.asarray(split_tables(modes, pixels, sims))
     vmem, smem = pl.BlockSpec(memory_space=pltpu.VMEM), pl.BlockSpec(memory_space=pltpu.SMEM)
-    out = jax.ShapeDtypeStruct((pairs, comps, padded), F32)
-    grad, curl = pl.pallas_call(
+    out = jax.ShapeDtypeStruct(tbar_alm.shape, F32)
+    return pl.pallas_call(
         functools.partial(fused_kernel, n, modes, rows, cycles, pixels, sims),
         out_shape=(out, out),
-        in_specs=[smem] * 4 + [vmem] * 6 + [pl.BlockSpec(memory_space=pl.ANY)],
+        in_specs=[smem] * 4 + [vmem] * 5 + [pl.BlockSpec(memory_space=pl.ANY)],
         out_specs=(vmem, vmem),
         scratch_shapes=[
             pltpu.VMEM(table.shape, BF16),
-            pltpu.VMEM((total, padded), BF16),
-            pltpu.VMEM((total, padded), BF16),
+            pltpu.VMEM((total, rows), BF16),
+            pltpu.VMEM((total, rows), BF16),
         ]
         + [pltpu.VMEM((n, 2 * pairs, LANES), BF16)] * 4
         + [pltpu.SemaphoreType.DMA]
@@ -459,11 +464,9 @@
         compiler_params=pltpu.CompilerParams(collective_id=0, has_side_effects=True),
         name="estimator",
     )(
-        m_slots, cycle_order, colatitude, cycle_weight, m_slots.reshape(1, -1), tbar, twf, leg,
-        prev, pixel_mask.reshape(pixels // LANES, LANES), table,
-    )
-    shape = (pairs, sims, 2, rows)
-    return grad[:, :, :rows].reshape(shape), curl[:, :, :rows].reshape(shape)
+        m_slots, cycle_order, colatitude, cycle_weight, m_slots.reshape(1, -1), tbar_alm,
+        twf_alm, by_cycle, pixel_mask.reshape(pixels // LANES, LANES), table,
+    )
 
 
 def body(n, *args):
@@ -478,6 +481,7 @@
         and rows <= 1025
         and (pixel_mask.shape[1] // LANES * sims) % LANES == 0
         and sims % 4 == 0
+        and all(v & (v - 1) == 0 for v in (sims, cycles, pixel_mask.shape[1]))
     )
     return fused(*args, n) if fits else shards(*args)
 

time: 25.4 us -> 21.2 us (0.83)
  local copies, waits for them, and re-layouts: 6.25 us -> 2.23 us
    reshape x4 -> x0, local copies, waits for them, and re-layouts: 3.21 us -> none  [the longest x2 2.32 us: fused(): return (grad[:, :, :rows].reshape(shape), curl[:, :, :rows].reshape(shape))]
    pad x4 -> x0, local copies, waits for them, and re-layouts: 2.66 us -> none  [the longest x1 0.74 us: fused(): jnp.pad(by_cycle[:, :, :rows - 1], ((0, 0), (0, 0), (1, padded - rows)))]
    unnamed x6 -> x4, local copies, waits for them, and re-layouts: 0.38 us -> 2.23 us
where the time goes in v2:
time: 21.2 us; the launch traced here: 21 us
  Pallas kernels  18.1 us (85%)
  local copies, waits for them, and re-layouts  2.23 us (11%)
  between operations  0.65 us (3%)
    pallas_call x1, Pallas kernels, fused(): pl.pallas_call(functools.partial(fused_kernel, n, modes, rows, cycles, pi...  18.1 us
    unnamed x4, local copies, waits for them, and re-layouts  2.23 us

profile of v2, /device:TPU:0, one launch (start us, length us, event | category | flops | bytes accessed | tf_op | source)
XLA Modules:
  0.0 21.0 jit_solution(6993427373143707530)
XLA Ops:
  0.6 18.1 %estimator.1 = (f32[8,4,2,257]{3,2,1,0:T(2,128)}, f32[8,4,2,257]{3,2,1,0:T(2,128)}) custom-call(s32[128]{0:T(128)} %slots_s.1, s32[16]{0:T(128)} %cycle_s.1, f32[16]{0:T(128)} %colat_s.1, f32[16]{0:T(128)} %weight_s.1, s32[1,128]{1,0:T(1,128)} %bitcast.5, bf16[8,4,2,257]{3,2,1,0:T(2,128)(2,1)} %tbar_ref.1, bf16[8,4,2,257]{3,2,1,0:T(2,128)(2,1)} %twf_ref.1, ...), custom_call_target="tpu_custom_call" | custom-call | tf_op jit(solution)/shard_map/estimator/pallas_call | solution.py:451
  18.7 0.0 copy-start
  18.7 1.6 %copy.13 = f32[8,4,2,257]{3,2,1,0:T(2,128)} copy(f32[8,4,2,257]{3,2,1,0:T(2,128)} %get-tuple-element.4) | data formatting | bytes 131584
  20.3 0.0 copy-done
  20.3 0.6 %copy.14 = f32[8,4,2,257]{3,2,1,0:T(2,128)} copy(f32[8,4,2,257]{3,2,1,0:T(2,128)S(1)} %copy-done) | data formatting | bytes 131584
Async XLA Ops:
  18.7 1.6 %copy-start = (f32[8,4,2,257]{3,2,1,0:T(2,128)S(1)}, f32[8,4,2,257]{3,2,1,0:T(2,128)}, u32[]{:S(2)}) copy-start(f32[8,4,2,257]{3,2,1,0:T(2,128)} %get-tuple-element.5) | copy-start | bytes 197380

commit v3 on v2

--- a/solution.py
+++ b/solution.py
@@ -447,7 +447,7 @@
     by_cycle = jnp.transpose(legendre, (0, 2, 1))
     table = jnp.asarray(split_tables(modes, pixels, sims))
     vmem, smem = pl.BlockSpec(memory_space=pltpu.VMEM), pl.BlockSpec(memory_space=pltpu.SMEM)
-    out = jax.ShapeDtypeStruct(tbar_alm.shape, F32)
+    out = pltpu.VMEM(tbar_alm.shape, F32)
     return pl.pallas_call(
         functools.partial(fused_kernel, n, modes, rows, cycles, pixels, sims),
         out_shape=(out, out),

time: 21.2 us -> 19.5 us (0.920)
  local copies, waits for them, and re-layouts: 2.23 us -> 1.28 us
  Pallas kernels: 18.1 us -> 17.4 us
    unnamed x4 -> x2, local copies, waits for them, and re-layouts: 2.23 us -> 1.28 us
    pallas_call x1, Pallas kernels: 18.1 us -> 17.4 us  [fused(): pl.pallas_call(functools.partial(fused_kernel, n, modes, rows, cycles, pi...]
where the time goes in v3:
time: 19.5 us; the launch traced here: 19.4 us
  Pallas kernels  17.4 us (89%)
  local copies, waits for them, and re-layouts  1.28 us (7%)
  between operations  0.64 us (3%)
    pallas_call x1, Pallas kernels, fused(): pl.pallas_call(functools.partial(fused_kernel, n, modes, rows, cycles, pi...  17.4 us
    unnamed x2, local copies, waits for them, and re-layouts  1.28 us

profile of v3, /device:TPU:0, one launch (start us, length us, event | category | flops | bytes accessed | tf_op | source)
XLA Modules:
  0.0 19.4 jit_solution(6484061834969632944)
XLA Ops:
  0.6 17.4 %estimator.1 = (f32[8,4,2,257]{3,2,1,0:T(2,128)S(1)}, f32[8,4,2,257]{3,2,1,0:T(2,128)S(1)}) custom-call(s32[128]{0:T(128)} %slots_s.1, s32[16]{0:T(128)} %cycle_s.1, f32[16]{0:T(128)} %colat_s.1, f32[16]{0:T(128)} %weight_s.1, s32[1,128]{1,0:T(1,128)} %bitcast.5, bf16[8,4,2,257]{3,2,1,0:T(2,128)(2,1)} %tbar_ref.1, bf16[8,4,2,257]{3,2,1,0:T(2,128)(2,1)} %twf_ref.1, ...), custom_call_target="tpu_custom_call" | custom-call | tf_op jit(solution)/shard_map/estimator/pallas_call | solution.py:451
  18.1 0.6 %copy.13 = f32[8,4,2,257]{3,2,1,0:T(2,128)} copy(f32[8,4,2,257]{3,2,1,0:T(2,128)S(1)} %get-tuple-element.2) | data formatting | bytes 131584
  18.7 0.6 %copy.14 = f32[8,4,2,257]{3,2,1,0:T(2,128)} copy(f32[8,4,2,257]{3,2,1,0:T(2,128)S(1)} %get-tuple-element.3) | data formatting | bytes 131584

commit v4 on v3

--- a/solution.py
+++ b/solution.py
@@ -220,10 +220,9 @@
 
 def fused_kernel(
     n, modes, rows, cycles, pixels, sims,
-    slots_s, cycle_s, colat_s, weight_s, slots_v, tbar_ref, twf_ref, leg_ref, mask_ref,
-    table_hbm, grad_ref, curl_ref,
-    table_v, leg_all, prev_all, send_f, recv_f, send_p, recv_p,
-    table_sem, fs_sem, fr_sem, ps_sem, pr_sem,
+    slots_s, cycle_s, colat_s, weight_s, slots_v, tbar_hbm, twf_hbm, leg_hbm, mask_hbm,
+    table_hbm, grad_ref, curl_ref, tbar_ref, twf_ref, leg_ref, mask_ref, table_v, leg_all, prev_all, send_f, recv_f, send_p, recv_p,
+    load_sem, fs_sem, fr_sem, ps_sem, pr_sem,
 ):
     me = lax.axis_index("ma")
     pairs, padded = tbar_ref.shape[0], rows
@@ -231,14 +230,22 @@
     comps = 2 * sims
     span = 2 * cycles
     total = pairs * span
-    fetch = pltpu.make_async_copy(table_hbm, table_v, table_sem)
-    fetch.start()
     barrier = pltpu.get_barrier_semaphore()
     for off in range(1, n):
         pl.semaphore_signal(
             barrier, inc=1, device_id={"ma": lax.rem(me + off, n)},
             device_id_type=pl.DeviceIdType.MESH,
         )
+
+    loads = [
+        pltpu.make_async_copy(source, target, load_sem.at[at])
+        for at, (source, target) in enumerate(
+            [(leg_hbm, leg_ref), (tbar_hbm, tbar_ref), (twf_hbm, twf_ref),
+             (table_hbm, table_v), (mask_hbm, mask_ref)]
+        )
+    ]
+    for load in loads:
+        load.start()
 
     row_shape = (pairs, padded)
     smaller = jnp.zeros(row_shape, jnp.int32)
@@ -265,6 +272,8 @@
 
     blank = jnp.zeros((comps, padded), F32)
     pieces = []
+    for load in loads[:3]:
+        load.wait()
     for p in range(pairs):
         tbar = jnp.concatenate([tbar_ref[p, s].astype(F32) for s in range(sims)], axis=0)
         twf = jnp.concatenate([twf_ref[p, s].astype(F32) for s in range(sims)], axis=0)
@@ -329,7 +338,8 @@
     select = one_hot(iota((modes, n * block), 0).astype(F32) == picked)
 
     hs = pixels // LANES * sims
-    fetch.wait()
+    for load in loads[3:]:
+        load.wait()
     moved = dot(table_v[...], select)
     fine_cos, fine_sin = moved[:LANES], moved[LANES : 2 * LANES]
     at = 2 * LANES
@@ -451,15 +461,19 @@
     return pl.pallas_call(
         functools.partial(fused_kernel, n, modes, rows, cycles, pixels, sims),
         out_shape=(out, out),
-        in_specs=[smem] * 4 + [vmem] * 5 + [pl.BlockSpec(memory_space=pl.ANY)],
+        in_specs=[smem] * 4 + [vmem] + [pl.BlockSpec(memory_space=pl.ANY)] * 5,
         out_specs=(vmem, vmem),
         scratch_shapes=[
+            pltpu.VMEM(tbar_alm.shape, BF16),
+            pltpu.VMEM(twf_alm.shape, BF16),
+            pltpu.VMEM(by_cycle.shape, BF16),
+            pltpu.VMEM((pixels // LANES, LANES), jnp.int32),
             pltpu.VMEM(table.shape, BF16),
             pltpu.VMEM((total, rows), BF16),
             pltpu.VMEM((total, rows), BF16),
         ]
         + [pltpu.VMEM((n, 2 * pairs, LANES), BF16)] * 4
-        + [pltpu.SemaphoreType.DMA]
+        + [pltpu.SemaphoreType.DMA((5,))]
         + [pltpu.SemaphoreType.DMA((n,))] * 4,
         compiler_params=pltpu.CompilerParams(collective_id=0, has_side_effects=True),
         name="estimator",

time: 19.5 us -> 19.3 us (0.990)
  Pallas kernels: 17.4 us -> 17.2 us
where the time goes in v4:
time: 19.3 us; the launch traced here: 19.2 us
  Pallas kernels  17.2 us (89%)
  local copies, waits for them, and re-layouts  1.28 us (7%)
  between operations  0.64 us (3%)
    pallas_call x1, Pallas kernels, fused(): pl.pallas_call(functools.partial(fused_kernel, n, modes, rows, cycles, pi...  17.2 us
    unnamed x2, local copies, waits for them, and re-layouts  1.28 us

profile of v4, /device:TPU:0, one launch (start us, length us, event | category | flops | bytes accessed | tf_op | source)
XLA Modules:
  0.0 19.2 jit_solution(15928283632376012097)
XLA Ops:
  0.6 17.2 %estimator.1 = (f32[8,4,2,257]{3,2,1,0:T(2,128)S(1)}, f32[8,4,2,257]{3,2,1,0:T(2,128)S(1)}) custom-call(s32[128]{0:T(128)} %slots_s.1, s32[16]{0:T(128)} %cycle_s.1, f32[16]{0:T(128)} %colat_s.1, f32[16]{0:T(128)} %weight_s.1, s32[1,128]{1,0:T(1,128)} %bitcast.5, bf16[8,4,2,257]{3,2,1,0:T(2,128)(2,1)} %tbar_hbm.1, bf16[8,4,2,257]{3,2,1,0:T(2,128)(2,1)} %twf_hbm.1, ...), custom_call_target="tpu_custom_call" | custom-call | tf_op jit(solution)/shard_map/estimator/pallas_call | solution.py:461
  17.9 0.6 %copy.13 = f32[8,4,2,257]{3,2,1,0:T(2,128)} copy(f32[8,4,2,257]{3,2,1,0:T(2,128)S(1)} %get-tuple-element.2) | data formatting | bytes 131584
  18.5 0.6 %copy.14 = f32[8,4,2,257]{3,2,1,0:T(2,128)} copy(f32[8,4,2,257]{3,2,1,0:T(2,128)S(1)} %get-tuple-element.3) | data formatting | bytes 131584
